TPU v7x, 32 devices: a whole 2x2x4 slice. The times are simulated.
32 devices in a mesh: ov: 16 (over z, y, core), vec: 2 (over x).
Axes of the slice: x: 2, y: 2, z: 4, core: 2. Of those that a mesh axis runs over, the one named last changes fastest.
Arguments:
- chol_vectors: bfloat16 [196608, 4096], P('ov', 'vec'), may hold values from -3.5 to 3.5
- amplitudes: bfloat16 [196608, 256], P('ov'), may hold values from -0.013671875 to 0.013671875
- sigma_prior: bfloat16 [196608, 256], P(('ov', 'vec')), may hold values from -4 to 4
Outputs:
- sigma_cycle: bfloat16 [196608, 256], P(('ov', 'vec'))
All inputs are finite; a program needn't handle non-finite values.
Results may differ from a plain program's by a relative error of at most 0.0065.
Values may be sent and summed in bfloat16 or wider, within the bound.
A program may use at most 128 MiB of HBM per device.

v0:
```python
import jax
import jax.numpy as jnp
from jax import lax
from jax.sharding import PartitionSpec as P


def body(chol_vectors, amplitudes, sigma_prior):
    contract = (((0,), (0,)), ((), ()))
    partial_x = lax.dot_general(
        chol_vectors, amplitudes, contract, preferred_element_type=jnp.float32
    )
    summed = lax.psum(partial_x, "ov")
    coupling = summed.astype(jnp.bfloat16)
    cycle = lax.psum_scatter(
        jnp.dot(chol_vectors, coupling, preferred_element_type=jnp.float32),
        "vec",
        scatter_dimension=0,
        tiled=True,
    )
    return (sigma_prior.astype(jnp.float32) + cycle).astype(jnp.bfloat16)


def solution(mesh):
    return jax.shard_map(
        body,
        mesh=mesh,
        in_specs=(P("ov", "vec"), P("ov", None), P(("ov", "vec"), None)),
        out_specs=P(("ov", "vec"), None),
        check_vma=False,
    )
```

profile of v0, /device:TPU:0, one launch (start us, length us, event | category | flops | bytes accessed | tf_op | source)
XLA Modules:
  0.0 287.8 jit_solution(18080904443797007626)
XLA Ops:
  6.5 0.0 reduce-scatter.2.cloned.1.call-start
  6.5 21.7 %fusion.1 = f32[2048,256]{1,0:T(8,128)S(1)} fusion(bf16[12288,2048]{1,0:T(8,128)(2,1)} %param.3, bf16[12288,256]{1,0:T(8,128)(2,1)} %param.4), kind=kOutput, calls=%fused_computation.3 | convolution fusion | flops 12884901888 | bytes 58720256 | tf_op jit(solution)/shard_map/dot_general | solution.py:9
  28.3 76.9 %all-reduce.1 = bf16[2048,256]{1,0:T(8,128)(2,1)S(1)} all-reduce(f32[2048,256]{1,0:T(8,128)S(1)} %fusion.1), channel_id=1, replica_groups=mesh['ov'=16,'vec'=2] {'ov'}, use_global_device_ids=true, to_apply=%region_0.0 | all-reduce | flops 524288 | bytes 3145728 | tf_op jit(solution)/shard_map/psum | solution.py:12
  105.1 23.9 %convolution_bitcast_fusion = f32[12288,256]{0,1:T(8,128)} fusion(bf16[12288,2048]{1,0:T(8,128)(2,1)} %param.3, bf16[2048,256]{1,0:T(8,128)(2,1)S(1)} %all-reduce.1), kind=kOutput, calls=%fused_computation | convolution fusion | flops 12884901888 | bytes 63963136 | tf_op jit(solution)/shard_map/dot_general | solution.py:15
  129.1 0.0 reduce-scatter.2.cloned.1.call-update
  129.1 3.2 %copy.4 = bf16[6144,256]{0,1:T(8,128)(2,1)S(1)} copy(bf16[6144,256]{1,0:T(8,128)(2,1)} %param.5) | data formatting | bytes 6291456 | tf_op args[2]
  132.3 138.7 %reduce-scatter.2.cloned.1.call-done = f32[6144,256]{0,1:T(8,128)} async-done(((f32[12288,256]{0,1:T(8,128)}), f32[6144,256]{0,1:T(8,128)}) %reduce-scatter.2.cloned.1.call-update) | async-done | bytes 6291472 | tf_op jit(solution)/shard_map/reduce_scatter | solution.py:14
  271.0 5.3 %add_convert_fusion = bf16[6144,256]{0,1:T(8,128)(2,1)} fusion(f32[6144,256]{0,1:T(8,128)} %reduce-scatter.2.cloned.1.call-done, bf16[6144,256]{0,1:T(8,128)(2,1)S(1)} %copy.4), kind=kLoop, calls=%fused_computation.1 | loop fusion | flops 4718592 | bytes 12582912 | tf_op jit(solution)/shard_map/convert_element_type | solution.py:20
  276.3 4.6 %copy.5 = bf16[6144,256]{1,0:T(8,128)(2,1)} copy(bf16[6144,256]{0,1:T(8,128)(2,1)} %add_convert_fusion) | data formatting | bytes 6291456 | tf_op jit(solution)/shard_map/convert_element_type | solution.py:20
Async XLA Ops:
  6.5 264.5 %reduce-scatter.2.cloned.1.call-start = ((), (), s32[]{:S(2)}) async-start(), calls=%async_computation.1 | async-start | bytes 18874368 | tf_op jit(solution)/shard_map/reduce_scatter | solution.py:14
Sparse Core Ops, SparseCore 0:
  129.2 141.7 reduce-scatter.1
where the time goes:
time: 288 us
  waiting for transfers between devices  139 us (48%)
  blocking collectives  76.9 us (27%)
  matrix products  45.6 us (16%)
  between operations  13.4 us (5%)
  local copies, waits for them, and re-layouts  7.82 us (3%)
  other arithmetic  5.28 us (2%)
    reduce_scatter x1, waiting for transfers between devices, body(): lax.psum_scatter(jnp.dot(chol_vectors, coupling, preferred_element_type=j...  139 us
    psum x1, blocking collectives, body(): summed = lax.psum(partial_x, 'ov')  76.9 us
    dot_general x1, matrix products, body(): jnp.dot(chol_vectors, coupling, preferred_element_type=jnp.float32)  23.9 us
    dot_general x1, matrix products, body(): lax.dot_general(chol_vectors, amplitudes, contract, preferred_element_typ...  21.7 us
  transfers between devices with their start and end apart: 1, of which 1 were waited for; matrix products, arithmetic and copies ran while one was open for 1% of the time, Pallas kernels for 0%

commit v1 on v0

--- a/solution.py
+++ b/solution.py
@@ -9,7 +9,7 @@
     partial_x = lax.dot_general(
         chol_vectors, amplitudes, contract, preferred_element_type=jnp.float32
     )
-    summed = lax.psum(partial_x, "ov")
+    summed = jnp.sum(lax.all_gather(partial_x, "ov"), axis=0)
     coupling = summed.astype(jnp.bfloat16)
     cycle = lax.psum_scatter(
         jnp.dot(chol_vectors, coupling, preferred_element_type=jnp.float32),

time: 288 us -> 400 us (1.39)
  waiting for transfers between devices: 139 us -> 312 us
  blocking collectives: 76.9 us -> 0 us
  other arithmetic: 5.28 us -> 17.4 us
    all_gather x0 -> x1, waiting for transfers between devices: none -> 171 us  [body(): summed = jnp.sum(lax.all_gather(partial_x, 'ov'), axis=0)]
    psum x1 -> x0, blocking collectives: 76.9 us -> none  [body(): summed = lax.psum(partial_x, 'ov')]
    reduce_sum x0 -> x1, other arithmetic: none -> 12.2 us  [body(): summed = jnp.sum(lax.all_gather(partial_x, 'ov'), axis=0)]
  transfers between devices with their start and end apart: 1 -> 2, of which waited for: 1 -> 2; matrix products, arithmetic and copies ran while one was open for 1% -> 1% of each run, Pallas kernels for 0% -> 0%
where the time goes in v1:
time: 400 us; the launch traced here: 399 us
  waiting for transfers between devices  312 us (78%)
  matrix products  48.1 us (12%)
  other arithmetic  17.4 us (4%)
  between operations  13.4 us (3%)
  local copies, waits for them, and re-layouts  7.82 us (2%)
    all_gather x1, waiting for transfers between devices, body(): summed = jnp.sum(lax.all_gather(partial_x, 'ov'), axis=0)  171 us
    reduce_scatter x1, waiting for transfers between devices, body(): lax.psum_scatter(jnp.dot(chol_vectors, coupling, preferred_element_type=j...  141 us
    dot_general x1, matrix products, body(): lax.dot_general(chol_vectors, amplitudes, contract, preferred_element_typ...  24.1 us
    dot_general x1, matrix products, body(): jnp.dot(chol_vectors, coupling, preferred_element_type=jnp.float32)  24 us
    reduce_sum x1, other arithmetic, body(): summed = jnp.sum(lax.all_gather(partial_x, 'ov'), axis=0)  12.2 us
  transfers between devices with their start and end apart: 2, of which 2 were waited for; matrix products, arithmetic and copies ran while one was open for 1% of the time, Pallas kernels for 0%

profile of v1, /device:TPU:0, one launch (start us, length us, event | category | flops | bytes accessed | tf_op | source)
XLA Modules:
  0.0 399.1 jit_solution(9852529187954831884)
XLA Ops:
  6.5 0.0 all-gather.3.cloned.1.call-start
  6.5 24.1 %fusion.1 = f32[2048,256]{1,0:T(8,128)} fusion(bf16[12288,2048]{1,0:T(8,128)(2,1)} %param.3, bf16[12288,256]{1,0:T(8,128)(2,1)} %param.4), kind=kOutput, calls=%fused_computation.3 | convolution fusion | flops 12884901888 | bytes 58720256 | tf_op jit(solution)/shard_map/dot_general | solution.py:9
  30.6 0.0 all-gather.3.cloned.1.call-update
  30.6 0.0 reduce-scatter.2.cloned.1.call-start
  30.7 170.9 %all-gather.3.cloned.1.call-done = f32[32768,256]{1,0:T(8,128)} async-done(((f32[2048,256]{1,0:T(8,128)}), f32[32768,256]{1,0:T(8,128)}) %all-gather.3.cloned.1.call-update) | async-done | bytes 33554448 | tf_op jit(solution)/shard_map/all_gather | solution.py:12
  201.5 12.2 %reduce_sum.9 = bf16[2048,256]{1,0:T(8,128)(2,1)S(1)} reduce(f32[16,2048,256]{2,1,0:T(8,128)} %bitcast.7, f32[]{:T(128)} %constant.0.clone.1), dimensions={0}, to_apply=%region_0.0 | reduce | flops 7864320 | bytes 34603012 | tf_op jit(solution)/shard_map/reduce_sum | solution.py:12
  213.7 24.0 %convolution_bitcast_fusion = f32[12288,256]{0,1:T(8,128)} fusion(bf16[12288,2048]{1,0:T(8,128)(2,1)} %param.3, bf16[2048,256]{1,0:T(8,128)(2,1)S(1)} %reduce_sum.9), kind=kOutput, calls=%fused_computation | convolution fusion | flops 12884901888 | bytes 63963136 | tf_op jit(solution)/shard_map/dot_general | solution.py:15
  237.7 0.0 reduce-scatter.2.cloned.1.call-update
  237.7 3.2 copy.4
  240.9 141.5 %reduce-scatter.2.cloned.1.call-done = f32[6144,256]{0,1:T(8,128)} async-done(((f32[12288,256]{0,1:T(8,128)}), f32[6144,256]{0,1:T(8,128)}) %reduce-scatter.2.cloned.1.call-update) | async-done | bytes 6291472 | tf_op jit(solution)/shard_map/reduce_scatter | solution.py:14
  382.4 5.3 %add_convert_fusion = bf16[6144,256]{0,1:T(8,128)(2,1)} fusion(f32[6144,256]{0,1:T(8,128)} %reduce-scatter.2.cloned.1.call-done, bf16[6144,256]{0,1:T(8,128)(2,1)S(1)} %copy.4), kind=kLoop, calls=%fused_computation.1 | loop fusion | flops 4718592 | bytes 12582912 | tf_op jit(solution)/shard_map/convert_element_type | solution.py:20
  387.7 4.6 %copy.5 = bf16[6144,256]{1,0:T(8,128)(2,1)} copy(bf16[6144,256]{0,1:T(8,128)(2,1)} %add_convert_fusion) | data formatting | bytes 6291456 | tf_op jit(solution)/shard_map/convert_element_type | solution.py:20
Async XLA Ops:
  6.5 195.0 %all-gather.3.cloned.1.call-start = ((), (), s32[]{:S(2)}) async-start(), calls=%async_computation.2 | async-start | bytes 35651584 | tf_op jit(solution)/shard_map/all_gather | solution.py:12
  30.6 351.8 %reduce-scatter.2.cloned.1.call-start = ((), (), s32[]{:S(2)}) async-start(), calls=%async_computation.1 | async-start | bytes 18874368 | tf_op jit(solution)/shard_map/reduce_scatter | solution.py:14
Sparse Core Ops, SparseCore 0:
  30.7 170.7 all-gather.2
  237.8 144.5 reduce-scatter.1
